TPU v7x, 256 devices: a 8x8x2 block of a 8x8x16 slice. The times are simulated.
256 devices in a mesh: groups: 2 (over z), cells: 128 (over y, x, core).
Axes of the slice: x: 8, y: 8, z: 2, core: 2. Of those that a mesh axis runs over, the one named last changes fastest.
The devices are a block of a 8x8x16 slice.
Arguments:
- pair_act: bfloat16 [768, 384, 128], P(('groups', 'cells')), parts along dimension 0, may hold values from -6 to 6
- pair_mask: int32 [768, 384], P(('groups', 'cells')), parts along dimension 0, may hold values from 0 to 1, as said below
- chain_ids: int32 [768], P('groups'), parts along dimension 0, may hold values from 0 to 3, never falling along the last dimension, each value on 1 to 192 neighbouring positions
- proj_weight: bfloat16 [128, 256], replicated, may hold values from -0.5 to 0.5
- gate_weight: bfloat16 [128, 128], replicated, may hold values from -0.5 to 0.5
- chain_bias: float32 [2, 128], replicated, may hold values from -4 to 4
- out_weight: bfloat16 [64, 128], replicated, may hold values from -0.75 to 0.75
- out_grad: bfloat16 [768, 384, 128], P(('groups', 'cells')), parts along dimension 0, may hold values from -6 to 6
Outputs:
- pair_grad: bfloat16 [768, 384, 128], P(('groups', 'cells')), parts along dimension 0
- proj_weight_grad: float32 [256, 256], P('groups'), parts along dimension 0
- gate_weight_grad: float32 [256, 128], P('groups'), parts along dimension 0
- out_weight_grad: float32 [128, 128], P('groups'), parts along dimension 0
There are 2 independent parts, one for each index of `groups`. A program takes and returns all parts, laid end to end along the dimension named above; an argument that names none is the same for every part. Nothing has to cross between parts.
Inputs may be any that keep to these rules, and one draw needn't show every extreme that they name: pair_mask[i, j] = valid[i] * valid[j] for a 0 or 1 validity of each residue.
All inputs are finite; a program needn't handle non-finite values.
Results may differ from a plain program's by a relative error of at most 0.012.
Values may be sent and summed in bfloat16 or wider, within the bound.
A program may use at most 64 MiB of HBM per device.

v0:
```python
import jax
import jax.numpy as jnp
from jax import lax
from jax.sharding import PartitionSpec as P

EPS = 1e-05


def in_one(arrays, axis):
    ends = [0]
    for a in arrays:
        ends.append(ends[-1] + a.size)
    subtotal = lax.psum(jnp.concatenate([a.ravel() for a in arrays]), axis)
    return tuple((subtotal[b:e].reshape(a.shape) for a, b, e in zip(arrays, ends, ends[1:])))


def normalize_axis(values, axis):
    center = values - jnp.mean(values, axis=axis, keepdims=True)
    scale = lax.rsqrt(jnp.mean(center * center, axis=axis, keepdims=True) + EPS)
    return (center * scale, scale)


def norm_backward(grad, normed, scale, axis):
    first = jnp.mean(grad, axis=axis, keepdims=True)
    second = jnp.mean(grad * normed, axis=axis, keepdims=True)
    return scale * (grad - first - normed * second)


def local(
    pair_act, pair_mask, chain_ids, proj_weight, gate_weight, chain_bias, out_weight, out_grad
):
    devices = lax.axis_size("cells")
    rows_here = pair_act.shape[0]
    length = pair_act.shape[1]
    width = pair_act.shape[2]
    hidden = out_weight.shape[0]
    halfway = length // 2
    channel_pairs = devices // 2
    per_device = 2 * hidden // devices
    count = rows_here * length
    zfull = pair_act.astype(jnp.float32).reshape(count, width)
    zhat, zscale = normalize_axis(zfull, 1)
    normed = zhat.astype(jnp.bfloat16)
    projected = jnp.einsum("xc,cf->fx", normed, proj_weight, preferred_element_type=jnp.float32)
    keeper = pair_mask.astype(jnp.float32).reshape(1, count)
    values = projected[: 2 * hidden]
    sigma = jax.nn.sigmoid(projected[2 * hidden :])
    factors = (keeper * sigma * values).astype(jnp.bfloat16)
    outgoing = factors.reshape(2, channel_pairs, per_device, rows_here, 2, halfway)
    outgoing = jnp.transpose(outgoing, (1, 4, 0, 2, 3, 5)).reshape(
        devices, 2, per_device, rows_here, halfway
    )
    arrived = lax.all_to_all(outgoing, "cells", split_axis=0, concat_axis=3, tiled=True)
    left_half = arrived[0, 0]
    right_half = arrived[0, 1]
    partial_value = jnp.einsum(
        "cik,cjk->cij", left_half, right_half, preferred_element_type=jnp.float32
    )
    landed = lax.all_to_all(
        partial_value.reshape(per_device, devices, rows_here, length).astype(jnp.bfloat16),
        "cells",
        split_axis=1,
        concat_axis=0,
        tiled=True,
    ).astype(jnp.float32)
    landed = landed.reshape(channel_pairs, 2, per_device, rows_here, length)
    triangle = jnp.sum(landed, axis=1).reshape(hidden, count)
    tri_hat, tri_scale = normalize_axis(triangle, 0)
    tri_low = tri_hat.astype(jnp.bfloat16)
    outputs = jnp.einsum("hx,hc->xc", tri_low, out_weight, preferred_element_type=jnp.float32)
    start = lax.axis_index("cells") * rows_here
    own_chain = lax.dynamic_slice_in_dim(chain_ids, start, rows_here, 0)
    same_chain = (own_chain[:, None] == chain_ids[None, :]).reshape(count, 1)
    logits = jnp.dot(normed, gate_weight, preferred_element_type=jnp.float32)
    logits = logits + jnp.where(same_chain, chain_bias[0][None, :], chain_bias[1][None, :])
    gating = jax.nn.sigmoid(logits)
    upstream = out_grad.reshape(count, width).astype(jnp.float32)
    d_outputs = (upstream * gating).astype(jnp.bfloat16)
    d_logits = (upstream * outputs * gating * (1.0 - gating)).astype(jnp.bfloat16)
    out_term = jnp.einsum("hx,xc->hc", tri_low, d_outputs, preferred_element_type=jnp.float32)
    gate_term = jnp.einsum("xc,xd->cd", normed, d_logits, preferred_element_type=jnp.float32)
    d_hat = jnp.einsum("xc,hc->hx", d_outputs, out_weight, preferred_element_type=jnp.float32)
    d_tri = norm_backward(d_hat, tri_hat, tri_scale, 0).astype(jnp.bfloat16)
    doubled = jnp.broadcast_to(
        d_tri.reshape(channel_pairs, 1, per_device, rows_here, length),
        (channel_pairs, 2, per_device, rows_here, length),
    )
    whole = lax.all_to_all(
        doubled.reshape(devices, per_device, rows_here, length),
        "cells",
        split_axis=0,
        concat_axis=2,
        tiled=True,
    )[0]
    d_left = jnp.einsum("cij,cjk->cik", whole, right_half, preferred_element_type=jnp.float32)
    d_right = jnp.einsum("cij,cik->cjk", whole, left_half, preferred_element_type=jnp.float32)
    d_pair = jnp.stack([d_left, d_right]).astype(jnp.bfloat16)
    returned = lax.all_to_all(
        d_pair.reshape(2, per_device, devices, rows_here, halfway),
        "cells",
        split_axis=2,
        concat_axis=2,
        tiled=True,
    )
    returned = returned.reshape(2, per_device, channel_pairs, 2, rows_here, halfway)
    d_factors = (
        jnp.transpose(returned, (0, 2, 1, 4, 3, 5)).reshape(2 * hidden, count).astype(jnp.float32)
    )
    d_values = d_factors * keeper * sigma
    d_gates = d_factors * keeper * values * sigma * (1.0 - sigma)
    d_proj = jnp.concatenate([d_values, d_gates], axis=0).astype(jnp.bfloat16)
    proj_term = jnp.einsum("xc,fx->cf", normed, d_proj, preferred_element_type=jnp.float32)
    d_normed = jnp.einsum("fx,cf->xc", d_proj, proj_weight, preferred_element_type=jnp.float32)
    d_normed = d_normed + jnp.einsum(
        "xd,cd->xc", d_logits, gate_weight, preferred_element_type=jnp.float32
    )
    pair_grad = (
        norm_backward(d_normed, zhat, zscale, 1)
        .astype(jnp.bfloat16)
        .reshape(rows_here, length, width)
    )
    proj_sum, gate_sum, out_sum = in_one((proj_term, gate_term, out_term), "cells")
    factor = 1.0 / length
    return (pair_grad, proj_sum * factor, gate_sum * factor, out_sum * factor)


def solution(mesh):
    placed = (
        P(("groups", "cells"), None, None),
        P(("groups", "cells"), None),
        P("groups"),
        P(),
        P(),
        P(),
        P(),
        P(("groups", "cells"), None, None),
    )
    return jax.shard_map(
        local,
        mesh=mesh,
        in_specs=placed,
        out_specs=(
            P(("groups", "cells"), None, None),
            P("groups", None),
            P("groups", None),
            P("groups", None),
        ),
        check_vma=False,
    )
```

profile of v0, /device:TPU:513, one launch (start us, length us, event | category | flops | bytes accessed | tf_op | source)
XLA Modules:
  0.0 339.7 jit_solution(11828793296574214934)
XLA Ops:
  7.2 1.2 convert_reduce_fusion
  8.4 1.4 multiply_reduce_fusion.1
  9.8 0.7 convert_element_type.85
  10.5 1.3 fusion.15
  12.7 1.1 copy.41
  13.8 27.4 %all-to-all-start = ((bf16[128,2,1,3,192]{4,1,3,2,0:T(2,128)(2,1)}), bf16[128,2,1,3,192]{4,1,3,2,0:T(2,128)(2,1)S(1)}, u32[]{:S(2)}, u32[]{:S(2)}) async-start(bf16[128,2,1,3,192]{4,1,3,2,0:T(2,128)(2,1)} %bitcast.4), calls=%async_computation | async-start | bytes 786432 | tf_op jit(solution)/shard_map/all_to_all | solution.py:53
  41.3 17.2 %all-to-all-done = bf16[128,2,1,3,192]{4,1,3,2,0:T(2,128)(2,1)S(1)} async-done(((bf16[128,2,1,3,192]{4,1,3,2,0:T(2,128)(2,1)}), bf16[128,2,1,3,192]{4,1,3,2,0:T(2,128)(2,1)S(1)}, u32[]{:S(2)}, u32[]{:S(2)}) %all-to-all-start) | async-done | bytes 294944 | tf_op jit(solution)/shard_map/all_to_all | solution.py:53
  58.5 1.5 fusion.38
  60.1 0.7 copy.57
  61.2 1.0 copy.47
  62.2 7.6 %all-to-all-start.1 = ((bf16[1,128,3,384]{3,2,0,1:T(4,128)(2,1)}), bf16[1,128,3,384]{3,2,0,1:T(4,128)(2,1)S(1)}, u32[]{:S(2)}, u32[]{:S(2)}) async-start(bf16[1,128,3,384]{3,2,0,1:T(4,128)(2,1)} %copy.47), calls=%async_computation.1 | async-start | bytes 786432 | tf_op jit(solution)/shard_map/all_to_all | solution.py:59
  69.9 1.2 fusion.10
  71.1 15.6 %all-to-all-done.1 = bf16[1,128,3,384]{3,2,0,1:T(4,128)(2,1)S(1)} async-done(((bf16[1,128,3,384]{3,2,0,1:T(4,128)(2,1)}), bf16[1,128,3,384]{3,2,0,1:T(4,128)(2,1)S(1)}, u32[]{:S(2)}, u32[]{:S(2)}) %all-to-all-start.1) | async-done | bytes 294944 | tf_op jit(solution)/shard_map/all_to_all | solution.py:59
  87.8 0.9 broadcast_in_dim.53
  88.6 7.4 %all-to-all-start.2 = ((bf16[128,1,3,384]{3,2,1,0:T(4,128)(2,1)}), bf16[128,1,3,384]{3,2,1,0:T(4,128)(2,1)S(1)}, u32[]{:S(2)}, u32[]{:S(2)}) async-start(bf16[128,1,3,384]{3,2,1,0:T(4,128)(2,1)} %bitcast.18), calls=%async_computation.2 | async-start | bytes 786432 | tf_op jit(solution)/shard_map/all_to_all | solution.py:88
  96.1 0.7 copy.56
  96.8 16.4 %all-to-all-done.2 = bf16[128,1,3,384]{3,2,1,0:T(4,128)(2,1)S(1)} async-done(((bf16[128,1,3,384]{3,2,1,0:T(4,128)(2,1)}), bf16[128,1,3,384]{3,2,1,0:T(4,128)(2,1)S(1)}, u32[]{:S(2)}, u32[]{:S(2)}) %all-to-all-start.2) | async-done | bytes 294944 | tf_op jit(solution)/shard_map/all_to_all | solution.py:88
  114.4 1.2 copy.53
  115.6 7.4 %all-to-all-start.3 = ((bf16[2,1,128,3,192]{4,0,3,1,2:T(2,128)(2,1)}), bf16[2,1,128,3,192]{4,0,3,1,2:T(2,128)(2,1)S(1)}, u32[]{:S(2)}, u32[]{:S(2)}) async-start(bf16[2,1,128,3,192]{4,0,3,1,2:T(2,128)(2,1)} %copy.53), calls=%async_computation.3 | async-start | bytes 786432 | tf_op jit(solution)/shard_map/all_to_all | solution.py:98
  123.5 1.4 fusion.6
  125.2 14.9 %all-to-all-done.3 = bf16[2,1,128,3,192]{4,0,3,1,2:T(2,128)(2,1)S(1)} async-done(((bf16[2,1,128,3,192]{4,0,3,1,2:T(2,128)(2,1)}), bf16[2,1,128,3,192]{4,0,3,1,2:T(2,128)(2,1)S(1)}, u32[]{:S(2)}, u32[]{:S(2)}) %all-to-all-start.3) | async-done | bytes 294944 | tf_op jit(solution)/shard_map/all_to_all | solution.py:98
  140.4 0.4 copy.54
  140.8 0.6 reshape.312
  142.0 0.4 fusion.16
  142.6 0.7 fusion.37
  143.4 0.7 pad_maximum_fusion.4
  144.2 1.4 multiply_convert_fusion
  145.6 182.7 %all-reduce.2.cloned.1.call-done = f32[57344]{0:T(1024)} async-done(((f32[57344]{0:T(1024)}), f32[57344]{0:T(1024)}) %all-reduce.2.cloned.1.call-update) | async-done | bytes 229392 | tf_op jit(solution)/shard_map/psum | solution.py:13
  328.3 0.9 slice_multiply_fusion
  329.3 0.7 mul.168
  329.9 1.4 fusion.32
  331.3 1.5 fusion.31
  (63 shorter events, 5.6 us)
Async XLA Ops:
  7.2 4.6 %copy-start = (bf16[128,256]{1,0:T(8,128)(2,1)S(1)}, bf16[128,256]{1,0:T(8,128)(2,1)}, u32[]{:S(2)}) copy-start(bf16[128,256]{1,0:T(8,128)(2,1)} %param.11) | copy-start | bytes 196612
  12.4 28.9 %copy-start.8 = (s32[384]{0:T(512)S(1)}, s32[384]{0:T(512)}, u32[]{:S(2)}) copy-start(s32[384]{0:T(512)} %param.10) | copy-start | bytes 4612
  13.8 44.7 %all-to-all-start = ((bf16[128,2,1,3,192]{4,1,3,2,0:T(2,128)(2,1)}), bf16[128,2,1,3,192]{4,1,3,2,0:T(2,128)(2,1)S(1)}, u32[]{:S(2)}, u32[]{:S(2)}) async-start(bf16[128,2,1,3,192]{4,1,3,2,0:T(2,128)(2,1)} %bitcast.4), calls=%async_computation | async-start | bytes 786432 | tf_op jit(solution)/shard_map/all_to_all | solution.py:53
  60.8 9.1 %copy-start.9 = (f32[2,128]{1,0:T(2,128)S(1)}, f32[2,128]{1,0:T(2,128)}, u32[]{:S(2)}) copy-start(f32[2,128]{1,0:T(2,128)} %param.13) | copy-start | bytes 3076
  60.8 9.1 %copy-start.2 = (bf16[3,384,128]{2,1,0:T(8,128)(2,1)S(1)}, bf16[3,384,128]{2,1,0:T(8,128)(2,1)}, u32[]{:S(2)}) copy-start(bf16[3,384,128]{2,1,0:T(8,128)(2,1)} %param.15) | copy-start | bytes 884740
  60.8 9.1 %copy-start.6 = (bf16[128,128]{1,0:T(8,128)(2,1)S(1)}, bf16[128,128]{1,0:T(8,128)(2,1)}, u32[]{:S(2)}) copy-start(bf16[128,128]{1,0:T(8,128)(2,1)} %param.12) | copy-start | bytes 98308
  62.2 24.5 %all-to-all-start.1 = ((bf16[1,128,3,384]{3,2,0,1:T(4,128)(2,1)}), bf16[1,128,3,384]{3,2,0,1:T(4,128)(2,1)S(1)}, u32[]{:S(2)}, u32[]{:S(2)}) async-start(bf16[1,128,3,384]{3,2,0,1:T(4,128)(2,1)} %copy.47), calls=%async_computation.1 | async-start | bytes 786432 | tf_op jit(solution)/shard_map/all_to_all | solution.py:59
  71.1 16.3 %copy-start.4 = (bf16[64,128]{1,0:T(8,128)(2,1)S(1)}, bf16[64,128]{1,0:T(8,128)(2,1)}, u32[]{:S(2)}) copy-start(bf16[64,128]{1,0:T(8,128)(2,1)} %param.14) | copy-start | bytes 49156
  88.6 24.5 %all-to-all-start.2 = ((bf16[128,1,3,384]{3,2,1,0:T(4,128)(2,1)}), bf16[128,1,3,384]{3,2,1,0:T(4,128)(2,1)S(1)}, u32[]{:S(2)}, u32[]{:S(2)}) async-start(bf16[128,1,3,384]{3,2,1,0:T(4,128)(2,1)} %bitcast.18), calls=%async_computation.2 | async-start | bytes 786432 | tf_op jit(solution)/shard_map/all_to_all | solution.py:88
  114.4 9.1 %copy-start.3 = (bf16[3,384,128]{2,1,0:T(8,128)(2,1)S(1)}, bf16[3,384,128]{2,1,0:T(8,128)(2,1)}, u32[]{:S(2)}) copy-start(bf16[3,384,128]{2,1,0:T(8,128)(2,1)} %param.15) | copy-start | bytes 884740
  114.4 9.1 %copy-start.5 = (bf16[64,128]{1,0:T(8,128)(2,1)S(1)}, bf16[64,128]{1,0:T(8,128)(2,1)}, u32[]{:S(2)}) copy-start(bf16[64,128]{1,0:T(8,128)(2,1)} %param.14) | copy-start | bytes 49156
  115.6 24.5 %all-to-all-start.3 = ((bf16[2,1,128,3,192]{4,0,3,1,2:T(2,128)(2,1)}), bf16[2,1,128,3,192]{4,0,3,1,2:T(2,128)(2,1)S(1)}, u32[]{:S(2)}, u32[]{:S(2)}) async-start(bf16[2,1,128,3,192]{4,0,3,1,2:T(2,128)(2,1)} %copy.53), calls=%async_computation.3 | async-start | bytes 786432 | tf_op jit(solution)/shard_map/all_to_all | solution.py:98
  123.0 205.3 %all-reduce.2.cloned.1.call-start = ((), (), s32[]{:S(2)}) async-start(), calls=%async_computation.4 | async-start | bytes 458752 | tf_op jit(solution)/shard_map/psum | solution.py:13
  141.7 1.0 copy-start.1
  141.7 1.0 copy-start.7
Sparse Core Ops, SparseCore 0:
  144.3 183.9 all-reduce.1
where the time goes:
time: 340 us
  waiting for transfers between devices  247 us (73%)
  starting transfers between devices  50.2 us (15%)
  between operations  14.5 us (4%)
  other arithmetic  12 us (4%)
  local copies, waits for them, and re-layouts  10.4 us (3%)
  matrix products  5.81 us (2%)
    psum x1, waiting for transfers between devices, in_one(): subtotal = lax.psum(jnp.concatenate([a.ravel() for a in arrays]), axis)  183 us
    all_to_all x1, starting transfers between devices, local(): lax.all_to_all(outgoing, 'cells', split_axis=0, concat_axis=3, tiled=True)  27.4 us
    all_to_all x1, waiting for transfers between devices, local(): lax.all_to_all(outgoing, 'cells', split_axis=0, concat_axis=3, tiled=True)  17.2 us
    all_to_all x1, waiting for transfers between devices, local(): lax.all_to_all(doubled.reshape(devices, per_device, rows_here, length), '...  16.4 us
    all_to_all x1, waiting for transfers between devices, local(): lax.all_to_all(partial_value.reshape(per_device, devices, rows_here, leng...  15.6 us
    all_to_all x1, waiting for transfers between devices, local(): lax.all_to_all(d_pair.reshape(2, per_device, devices, rows_here, halfway)...  14.9 us
    all_to_all x1, starting transfers between devices, local(): lax.all_to_all(partial_value.reshape(per_device, devices, rows_here, leng...  7.62 us
    all_to_all x1, starting transfers between devices, local(): lax.all_to_all(d_pair.reshape(2, per_device, devices, rows_here, halfway)...  7.44 us
  transfers between devices with their start and end apart: 5, of which 5 were waited for; matrix products, arithmetic and copies ran while one was open for 2% of the time, Pallas kernels for 0%

commit v1 on v0

--- a/solution.py
+++ b/solution.py
@@ -10,7 +10,9 @@
     ends = [0]
     for a in arrays:
         ends.append(ends[-1] + a.size)
-    subtotal = lax.psum(jnp.concatenate([a.ravel() for a in arrays]), axis)
+    part = jnp.concatenate([a.ravel() for a in arrays])
+    terms = lax.all_gather(part, axis, axis=0, tiled=False)
+    subtotal = terms.sum(axis=0)
     return tuple((subtotal[b:e].reshape(a.shape) for a, b, e in zip(arrays, ends, ends[1:])))
 
 

time: 340 us -> 319 us (0.938)
  waiting for transfers between devices: 247 us -> 187 us
  local copies, waits for them, and re-layouts: 10.4 us -> 38.2 us
  other arithmetic: 12 us -> 21 us
    psum x1 -> x0, waiting for transfers between devices: 183 us -> none  [in_one(): subtotal = lax.psum(jnp.concatenate([a.ravel() for a in arrays]), axis)]
    all_gather x0 -> x1, waiting for transfers between devices: none -> 124 us  [in_one(): terms = lax.all_gather(part, axis, axis=0, tiled=False)]
    all_gather x0 -> x1, local copies, waits for them, and re-layouts: none -> 26 us  [in_one(): terms = lax.all_gather(part, axis, axis=0, tiled=False)]
    reduce_sum x0 -> x1, other arithmetic: none -> 10.9 us  [in_one(): subtotal = terms.sum(axis=0)]
where the time goes in v1:
time: 319 us; the launch traced here: 318 us
  waiting for transfers between devices  187 us (59%)
  starting transfers between devices  50.4 us (16%)
  local copies, waits for them, and re-layouts  38.2 us (12%)
  other arithmetic  21 us (7%)
  between operations  14.5 us (5%)
  matrix products  6.44 us (2%)
    all_gather x1, waiting for transfers between devices, in_one(): terms = lax.all_gather(part, axis, axis=0, tiled=False)  124 us
    all_to_all x1, starting transfers between devices, local(): lax.all_to_all(outgoing, 'cells', split_axis=0, concat_axis=3, tiled=True)  27.4 us
    all_gather x1, local copies, waits for them, and re-layouts, in_one(): terms = lax.all_gather(part, axis, axis=0, tiled=False)  26 us
    all_to_all x1, waiting for transfers between devices, local(): lax.all_to_all(outgoing, 'cells', split_axis=0, concat_axis=3, tiled=True)  17.2 us
    all_to_all x1, waiting for transfers between devices, local(): lax.all_to_all(doubled.reshape(devices, per_device, rows_here, length), '...  16.4 us
    all_to_all x1, waiting for transfers between devices, local(): lax.all_to_all(partial_value.reshape(per_device, devices, rows_here, leng...  15.6 us
    all_to_all x1, waiting for transfers between devices, local(): lax.all_to_all(d_pair.reshape(2, per_device, devices, rows_here, halfway)...  14.3 us
    reduce_sum x1, other arithmetic, in_one(): subtotal = terms.sum(axis=0)  10.9 us
  transfers between devices with their start and end apart: 5, of which 5 were waited for; matrix products, arithmetic and copies ran while one was open for 2% of the time, Pallas kernels for 0%

profile of v1, /device:TPU:513, one launch (start us, length us, event | category | flops | bytes accessed | tf_op | source)
XLA Modules:
  0.0 317.9 jit_solution(9246106325863713001)
XLA Ops:
  7.2 1.2 convert_reduce_fusion
  8.4 1.4 multiply_reduce_fusion.1
  9.8 0.7 convert_element_type.85
  10.5 1.3 fusion.15
  12.7 1.1 copy.55
  13.8 27.4 %all-to-all-start = ((bf16[128,2,1,3,192]{4,1,3,2,0:T(2,128)(2,1)}), bf16[128,2,1,3,192]{4,1,3,2,0:T(2,128)(2,1)S(1)}, u32[]{:S(2)}, u32[]{:S(2)}) async-start(bf16[128,2,1,3,192]{4,1,3,2,0:T(2,128)(2,1)} %bitcast.4), calls=%async_computation | async-start | bytes 786432 | tf_op jit(solution)/shard_map/all_to_all | solution.py:55
  41.4 17.2 %all-to-all-done = bf16[128,2,1,3,192]{4,1,3,2,0:T(2,128)(2,1)S(1)} async-done(((bf16[128,2,1,3,192]{4,1,3,2,0:T(2,128)(2,1)}), bf16[128,2,1,3,192]{4,1,3,2,0:T(2,128)(2,1)S(1)}, u32[]{:S(2)}, u32[]{:S(2)}) %all-to-all-start) | async-done | bytes 294944 | tf_op jit(solution)/shard_map/all_to_all | solution.py:55
  58.6 1.5 fusion.38
  60.2 0.7 copy.71
  61.2 1.0 copy.61
  62.2 7.6 %all-to-all-start.1 = ((bf16[1,128,3,384]{3,2,0,1:T(4,128)(2,1)}), bf16[1,128,3,384]{3,2,0,1:T(4,128)(2,1)S(1)}, u32[]{:S(2)}, u32[]{:S(2)}) async-start(bf16[1,128,3,384]{3,2,0,1:T(4,128)(2,1)} %copy.61), calls=%async_computation.1 | async-start | bytes 786432 | tf_op jit(solution)/shard_map/all_to_all | solution.py:61
  70.0 1.2 fusion.10
  71.1 15.6 %all-to-all-done.1 = bf16[1,128,3,384]{3,2,0,1:T(4,128)(2,1)S(1)} async-done(((bf16[1,128,3,384]{3,2,0,1:T(4,128)(2,1)}), bf16[1,128,3,384]{3,2,0,1:T(4,128)(2,1)S(1)}, u32[]{:S(2)}, u32[]{:S(2)}) %all-to-all-start.1) | async-done | bytes 294944 | tf_op jit(solution)/shard_map/all_to_all | solution.py:61
  87.8 0.9 broadcast_in_dim.53
  88.7 7.4 %all-to-all-start.2 = ((bf16[128,1,3,384]{3,2,1,0:T(4,128)(2,1)}), bf16[128,1,3,384]{3,2,1,0:T(4,128)(2,1)S(1)}, u32[]{:S(2)}, u32[]{:S(2)}) async-start(bf16[128,1,3,384]{3,2,1,0:T(4,128)(2,1)} %bitcast.18), calls=%async_computation.2 | async-start | bytes 786432 | tf_op jit(solution)/shard_map/all_to_all | solution.py:90
  96.1 0.7 copy.70
  96.8 16.4 %all-to-all-done.2 = bf16[128,1,3,384]{3,2,1,0:T(4,128)(2,1)S(1)} async-done(((bf16[128,1,3,384]{3,2,1,0:T(4,128)(2,1)}), bf16[128,1,3,384]{3,2,1,0:T(4,128)(2,1)S(1)}, u32[]{:S(2)}, u32[]{:S(2)}) %all-to-all-start.2) | async-done | bytes 294944 | tf_op jit(solution)/shard_map/all_to_all | solution.py:90
  113.4 0.9 copy.65
  114.3 1.1 reshape.304
  116.0 1.2 copy.67
  117.2 7.6 %all-to-all-start.3 = ((bf16[2,1,128,3,192]{4,0,3,1,2:T(2,128)(2,1)}), bf16[2,1,128,3,192]{4,0,3,1,2:T(2,128)(2,1)S(1)}, u32[]{:S(2)}, u32[]{:S(2)}) async-start(bf16[2,1,128,3,192]{4,0,3,1,2:T(2,128)(2,1)} %copy.67), calls=%async_computation.3 | async-start | bytes 786432 | tf_op jit(solution)/shard_map/all_to_all | solution.py:100
  125.3 1.4 fusion.6
  126.7 0.9 convolution_bitcast_fusion.1
  127.6 14.3 %all-to-all-done.3 = bf16[2,1,128,3,192]{4,0,3,1,2:T(2,128)(2,1)S(1)} async-done(((bf16[2,1,128,3,192]{4,0,3,1,2:T(2,128)(2,1)}), bf16[2,1,128,3,192]{4,0,3,1,2:T(2,128)(2,1)S(1)}, u32[]{:S(2)}, u32[]{:S(2)}) %all-to-all-start.3) | async-done | bytes 294944 | tf_op jit(solution)/shard_map/all_to_all | solution.py:100
  143.2 0.9 multiply_convert_fusion.2
  144.9 0.7 pad_maximum_fusion.4
  146.1 0.7 fusion.37
  146.9 1.4 multiply_convert_fusion
  148.2 123.9 %all-gather.3.cloned.1.call-done = f32[7340032]{0:T(1024)} async-done(((f32[57344]{0:T(1024)}), f32[7340032]{0:T(1024)}) %all-gather.3.cloned.1.call-update) | async-done | bytes 29360144 | tf_op jit(solution)/shard_map/all_gather | solution.py:14
  272.1 26.0 %reshape.314 = f32[128,57344]{1,0:T(8,128)} reshape(f32[7340032]{0:T(1024)} %all-gather.3.cloned.1.call-done) | data formatting | bytes 58720256 | tf_op jit(solution)/shard_map/all_gather | solution.py:14
  298.1 10.9 %reduce_sum.99 = f32[57344]{0:T(1024)S(1)} reduce(f32[128,57344]{1,0:T(8,128)} %reshape.314, f32[]{:T(128)} %constant.10.clone.1), dimensions={0}, to_apply=%region_9.10 | reduce | flops 7282688 | bytes 29589508 | tf_op jit(solution)/shard_map/reduce_sum | solution.py:15
  310.3 0.7 mul.168
  (69 shorter events, 7.6 us)
Async XLA Ops:
  7.2 4.7 %copy-start = (bf16[128,256]{1,0:T(8,128)(2,1)S(1)}, bf16[128,256]{1,0:T(8,128)(2,1)}, u32[]{:S(2)}) copy-start(bf16[128,256]{1,0:T(8,128)(2,1)} %param.11) | copy-start | bytes 196612
  10.5 1.7 copy-start.6
  12.4 28.9 %copy-start.10 = (s32[384]{0:T(512)S(1)}, s32[384]{0:T(512)}, u32[]{:S(2)}) copy-start(s32[384]{0:T(512)} %param.10) | copy-start | bytes 4612
  13.8 44.7 %all-to-all-start = ((bf16[128,2,1,3,192]{4,1,3,2,0:T(2,128)(2,1)}), bf16[128,2,1,3,192]{4,1,3,2,0:T(2,128)(2,1)S(1)}, u32[]{:S(2)}, u32[]{:S(2)}) async-start(bf16[128,2,1,3,192]{4,1,3,2,0:T(2,128)(2,1)} %bitcast.4), calls=%async_computation | async-start | bytes 786432 | tf_op jit(solution)/shard_map/all_to_all | solution.py:55
  60.9 9.0 %copy-start.11 = (f32[2,128]{1,0:T(2,128)S(1)}, f32[2,128]{1,0:T(2,128)}, u32[]{:S(2)}) copy-start(f32[2,128]{1,0:T(2,128)} %param.13) | copy-start | bytes 3076
  60.9 9.0 %copy-start.3 = (bf16[3,384,128]{2,1,0:T(8,128)(2,1)S(1)}, bf16[3,384,128]{2,1,0:T(8,128)(2,1)}, u32[]{:S(2)}) copy-start(bf16[3,384,128]{2,1,0:T(8,128)(2,1)} %param.15) | copy-start | bytes 884740
  60.9 9.0 %copy-start.8 = (bf16[128,128]{1,0:T(8,128)(2,1)S(1)}, bf16[128,128]{1,0:T(8,128)(2,1)}, u32[]{:S(2)}) copy-start(bf16[128,128]{1,0:T(8,128)(2,1)} %param.12) | copy-start | bytes 98308
  62.2 24.5 %all-to-all-start.1 = ((bf16[1,128,3,384]{3,2,0,1:T(4,128)(2,1)}), bf16[1,128,3,384]{3,2,0,1:T(4,128)(2,1)S(1)}, u32[]{:S(2)}, u32[]{:S(2)}) async-start(bf16[1,128,3,384]{3,2,0,1:T(4,128)(2,1)} %copy.61), calls=%async_computation.1 | async-start | bytes 786432 | tf_op jit(solution)/shard_map/all_to_all | solution.py:61
  71.1 16.3 %copy-start.7 = (bf16[64,128]{1,0:T(8,128)(2,1)S(1)}, bf16[64,128]{1,0:T(8,128)(2,1)}, u32[]{:S(2)}) copy-start(bf16[64,128]{1,0:T(8,128)(2,1)} %param.14) | copy-start | bytes 49156
  88.7 24.5 %all-to-all-start.2 = ((bf16[128,1,3,384]{3,2,1,0:T(4,128)(2,1)}), bf16[128,1,3,384]{3,2,1,0:T(4,128)(2,1)S(1)}, u32[]{:S(2)}, u32[]{:S(2)}) async-start(bf16[128,1,3,384]{3,2,1,0:T(4,128)(2,1)} %bitcast.18), calls=%async_computation.2 | async-start | bytes 786432 | tf_op jit(solution)/shard_map/all_to_all | solution.py:90
  117.2 8.1 %copy-start.4 = (bf16[3,384,128]{2,1,0:T(8,128)(2,1)S(1)}, bf16[3,384,128]{2,1,0:T(8,128)(2,1)}, u32[]{:S(2)}) copy-start(bf16[3,384,128]{2,1,0:T(8,128)(2,1)} %param.15) | copy-start | bytes 884740
  117.2 24.6 %all-to-all-start.3 = ((bf16[2,1,128,3,192]{4,0,3,1,2:T(2,128)(2,1)}), bf16[2,1,128,3,192]{4,0,3,1,2:T(2,128)(2,1)S(1)}, u32[]{:S(2)}, u32[]{:S(2)}) async-start(bf16[2,1,128,3,192]{4,0,3,1,2:T(2,128)(2,1)} %copy.67), calls=%async_computation.3 | async-start | bytes 786432 | tf_op jit(solution)/shard_map/all_to_all | solution.py:100
  124.8 147.3 %all-gather.3.cloned.1.call-start = ((), (), s32[]{:S(2)}) async-start(), calls=%async_computation.4 | async-start | bytes 29589504 | tf_op jit(solution)/shard_map/all_gather | solution.py:14
  144.1 0.8 copy-start.5
  144.5 1.6 copy-start.2
  144.5 1.6 copy-start.9
  298.1 12.9 %copy-start.1 = (bf16[128,256]{1,0:T(8,128)(2,1)S(1)}, bf16[128,256]{1,0:T(8,128)(2,1)}, u32[]{:S(2)}) copy-start(bf16[128,256]{1,0:T(8,128)(2,1)} %param.11) | copy-start | bytes 196612
Sparse Core Ops, SparseCore 0:
  145.8 126.2 all-gather.2
